TPU v7x, 16 devices: a whole 2x2x2 slice. The times are simulated.
16 devices in a mesh: dp: 4 (over z, y), tp: 4 (over x, core).
Axes of the slice: x: 2, y: 2, z: 2, core: 2. Of those that a mesh axis runs over, the one named last changes fastest.
Arguments:
- hidden: bfloat16 [64, 1024], P('dp'), parts along dimension 0
- lengths: int32 [64], P('dp'), parts along dimension 0
- choice: int32 [2, 64, 8], P(None, 'dp'), parts along dimension 1
- keys_one: bfloat16 [64, 64, 8, 64], P('dp', 'tp'), parts along dimension 0
- vals_one: bfloat16 [64, 64, 8, 64], P('dp', 'tp'), parts along dimension 0
- keys_two: bfloat16 [64, 64, 8, 64], P('dp', 'tp'), parts along dimension 0
- vals_two: bfloat16 [64, 64, 8, 64], P('dp', 'tp'), parts along dimension 0
- g_attn: bfloat16 [2, 1024], replicated
- w_q: bfloat16 [2, 1024, 1024], P(None, None, 'tp')
- w_k: bfloat16 [2, 1024, 512], P(None, None, 'tp')
- w_v: bfloat16 [2, 1024, 512], P(None, None, 'tp')
- w_o: bfloat16 [2, 1024, 1024], P(None, 'tp')
- g_mlp: bfloat16 [2, 1024], replicated
- w_router: bfloat16 [2, 1024, 32], replicated
- w_gate: bfloat16 [2, 32, 1024, 512], P(None, None, None, 'tp')
- w_up: bfloat16 [2, 32, 1024, 512], P(None, None, None, 'tp')
- w_down: bfloat16 [2, 32, 512, 1024], P(None, None, 'tp')
Outputs:
- output 1: bfloat16 [64, 1024], P('dp'), parts along dimension 0
- output 2: bfloat16 [64, 64, 8, 64], P('dp', None, 'tp'), parts along dimension 0
- output 3: bfloat16 [64, 64, 8, 64], P('dp', None, 'tp'), parts along dimension 0
- output 4: bfloat16 [64, 64, 8, 64], P('dp', None, 'tp'), parts along dimension 0
- output 5: bfloat16 [64, 64, 8, 64], P('dp', None, 'tp'), parts along dimension 0
There are 4 independent parts. A program takes and returns all parts, laid end to end along the dimension named above; an argument that names none is the same for every part.
All inputs are finite; a program needn't handle non-finite values.
Results may differ from a plain program's by a relative error of at most 0.02.
Values are sent between devices in bfloat16 or wider.
A program may use at most 1 GiB of HBM per device.

v0:
```python
import jax
import jax.numpy as jnp
from jax import lax
from jax.sharding import PartitionSpec as P

EPS = 1e-5
THETA = 1000000.0


def rms_norm(tensor, gain_vec):
    tensor_f = tensor.astype(jnp.float32)
    scale = lax.rsqrt(jnp.mean(tensor_f * tensor_f, axis=-1, keepdims=True) + EPS)
    return (tensor_f * scale * gain_vec.astype(jnp.float32)).astype(jnp.bfloat16)


def apply_rope(tensor, lengths):
    head_dim = tensor.shape[-1]
    half_dim = head_dim // 2
    inv_freq = THETA ** (-2.0 * jnp.arange(half_dim, dtype=jnp.float32) / head_dim)
    angle = lengths.astype(jnp.float32)[:, None] * inv_freq[None, :]
    cos_part = jnp.cos(angle)[:, None, :]
    sin_part = jnp.sin(angle)[:, None, :]
    lower_half = tensor[..., :half_dim]
    upper_half = tensor[..., half_dim:]
    return jnp.concatenate([lower_half * cos_part - upper_half * sin_part, upper_half * cos_part + lower_half * sin_part], axis=-1)


def expert_block(x_mid, choice, g_mlp, w_router, w_gate, w_up, w_down):
    normed = rms_norm(x_mid, g_mlp)
    logits = jnp.dot(normed, w_router, preferred_element_type=jnp.float32)
    onehot = (choice[:, :, None] == jnp.arange(w_router.shape[1])[None, None, :]).astype(jnp.float32)
    gate_prob = jax.nn.softmax(jnp.sum(onehot * logits[:, None, :], axis=-1), axis=-1)
    gate_mat = jnp.sum(gate_prob[:, :, None] * onehot, axis=1)
    gate_act = jnp.einsum('bd,edf->bef', normed, w_gate, preferred_element_type=jnp.float32)
    up_act = jnp.einsum('bd,edf->bef', normed, w_up, preferred_element_type=jnp.float32)
    expert_in = (jax.nn.silu(gate_act) * up_act * gate_mat[:, :, None]).astype(jnp.bfloat16)
    return jnp.einsum('bef,efd->bd', expert_in, w_down, preferred_element_type=jnp.float32)


def decode_layer(hidden, lengths, choice, key_cache, val_cache, g_attn, w_q, w_k, w_v, w_o, g_mlp, w_router, w_gate, w_up, w_down):
    batch_rows, seq_len, kv_heads, head_dim = key_cache.shape
    num_heads = w_q.shape[1] // head_dim
    normed = rms_norm(hidden, g_attn)
    query_rot = apply_rope(jnp.dot(normed, w_q, preferred_element_type=jnp.float32).reshape(batch_rows, num_heads, head_dim), lengths).astype(jnp.bfloat16)
    key_new = apply_rope(jnp.dot(normed, w_k, preferred_element_type=jnp.float32).reshape(batch_rows, kv_heads, head_dim), lengths).astype(jnp.bfloat16)
    val_new = jnp.dot(normed, w_v, preferred_element_type=jnp.float32).astype(jnp.bfloat16).reshape(batch_rows, kv_heads, head_dim)
    positions = jnp.arange(seq_len)
    is_new = (positions[None, :] == lengths[:, None])[:, :, None, None]
    key_cache = jnp.where(is_new, key_new[:, None], key_cache)
    val_cache = jnp.where(is_new, val_new[:, None], val_cache)
    query_grp = query_rot.reshape(batch_rows, kv_heads, num_heads // kv_heads, head_dim)
    scores = jnp.einsum('bgrd,bsgd->bgrs', query_grp, key_cache, preferred_element_type=jnp.float32) * head_dim ** -0.5
    is_valid = (positions[None, :] <= lengths[:, None])[:, None, None, :]
    attn_prob = jax.nn.softmax(jnp.where(is_valid, scores, -1e30), axis=-1).astype(jnp.bfloat16)
    attn_vec = jnp.einsum('bgrs,bsgd->bgrd', attn_prob, val_cache, preferred_element_type=jnp.float32).astype(jnp.bfloat16).reshape(batch_rows, num_heads * head_dim)
    attn_sum = lax.psum(jnp.dot(attn_vec, w_o, preferred_element_type=jnp.float32).astype(jnp.bfloat16), 'tp')
    x_mid = (hidden.astype(jnp.float32) + attn_sum.astype(jnp.float32)).astype(jnp.bfloat16)
    moe_sum = lax.psum(expert_block(x_mid, choice, g_mlp, w_router, w_gate, w_up, w_down).astype(jnp.bfloat16), 'tp')
    return (x_mid.astype(jnp.float32) + moe_sum.astype(jnp.float32)).astype(jnp.bfloat16), key_cache, val_cache


def solution(mesh):
    seq_spec = P('dp', 'tp', None, None)
    head_spec = P('dp', None, 'tp', None)
    col_spec = P(None, None, 'tp')
    ff_spec = P(None, None, None, 'tp')

    def local_step(hidden, lengths, choice, keys_one, vals_one, keys_two, vals_two, g_attn, w_q, w_k, w_v, w_o, g_mlp, w_router, w_gate, w_up, w_down):
        moved = [lax.all_to_all(cache_blk, 'tp', 2, 1, tiled=True) for cache_blk in (keys_one, vals_one, keys_two, vals_two)]
        results = []
        for layer_idx in range(2):
            hidden, key_cache, val_cache = decode_layer(hidden, lengths, choice[layer_idx], moved[2 * layer_idx], moved[2 * layer_idx + 1], g_attn[layer_idx], w_q[layer_idx], w_k[layer_idx], w_v[layer_idx], w_o[layer_idx], g_mlp[layer_idx], w_router[layer_idx], w_gate[layer_idx], w_up[layer_idx], w_down[layer_idx])
            results.append(key_cache)
            results.append(val_cache)
        return (hidden, results[0], results[1], results[2], results[3])

    return jax.shard_map(local_step, mesh=mesh, in_specs=(P('dp', None), P('dp'), P(None, 'dp', None), seq_spec, seq_spec, seq_spec, seq_spec, P(), col_spec, col_spec, col_spec, P(None, 'tp', None), P(), P(), ff_spec, ff_spec, P(None, None, 'tp', None)), out_specs=(P('dp', None), head_spec, head_spec, head_spec, head_spec), check_vma=False)
```

profile of v0, /device:TPU:0, one launch (start us, length us, event | category | flops | bytes accessed | tf_op | source)
XLA Modules:
  0.0 129.5 jit_solution(13767836649446918666)
XLA Ops:
  0.7 1.2 copy.115
  1.9 1.1 reshape.280
  3.0 4.5 %all-to-all-start = ((bf16[4,2,16384]{2,1,0:T(2,128)(2,1)}), bf16[4,2,16384]{2,1,0:T(2,128)(2,1)S(1)}, u32[]{:S(2)}, u32[]{:S(2)}) async-start(bf16[4,2,16384]{2,1,0:T(2,128)(2,1)} %reshape.280), calls=%async_computation | async-start | bytes 524288 | tf_op jit(solution)/shard_map/all_to_all | solution.py:69
  7.5 0.8 slice_convert_fusion.1
  8.2 0.9 fusion.86
  9.1 1.1 slice_bitcast_fusion.2
  10.4 0.7 convert_element_type.120
  11.1 1.0 fusion.118
  12.3 1.2 convolution_convert_fusion.5
  13.6 1.1 copy.114
  14.7 1.1 reshape.278
  15.8 1.3 slice_bitcast_fusion
  17.3 1.1 fusion.120
  18.5 0.6 copy.68
  19.1 0.7 slice_bitcast_fusion.4
  20.2 1.1 copy.113
  21.4 1.1 reshape.282
  22.5 1.1 copy.112
  23.6 1.1 reshape.276
  24.7 0.8 slice_convert_fusion.2
  25.5 3.4 %all-to-all-start.1 = ((bf16[4,2,16384]{2,1,0:T(2,128)(2,1)}), bf16[4,2,16384]{2,1,0:T(2,128)(2,1)S(1)}, u32[]{:S(2)}, u32[]{:S(2)}) async-start(bf16[4,2,16384]{2,1,0:T(2,128)(2,1)} %reshape.278), calls=%async_computation.1 | async-start | bytes 524288 | tf_op jit(solution)/shard_map/all_to_all | solution.py:69
  28.9 1.3 %iota_compare_fusion.3 = (pred[16,64]{1,0:T(8,128)(4,1)}, pred[16,64]{1,0:T(8,128)(4,1)S(1)}) fusion(s32[16]{0:T(128)} %param.18), kind=kLoop, calls=%fused_computation.155 | loop fusion | flops 2048 | bytes 2112 | tf_op jit(solution)/shard_map/le | solution.py:53
  30.6 0.5 copy.72
  31.2 3.6 %all-to-all-done.1 = bf16[4,2,16384]{2,1,0:T(2,128)(2,1)S(1)} async-done(((bf16[4,2,16384]{2,1,0:T(2,128)(2,1)}), bf16[4,2,16384]{2,1,0:T(2,128)(2,1)S(1)}, u32[]{:S(2)}, u32[]{:S(2)}) %all-to-all-start.1) | async-done | bytes 262176 | tf_op jit(solution)/shard_map/all_to_all | solution.py:69
  34.7 3.4 %all-to-all-start.2 = ((bf16[4,2,16384]{2,1,0:T(2,128)(2,1)}), bf16[4,2,16384]{2,1,0:T(2,128)(2,1)S(1)}, u32[]{:S(2)}, u32[]{:S(2)}) async-start(bf16[4,2,16384]{2,1,0:T(2,128)(2,1)} %reshape.282), calls=%async_computation.2 | async-start | bytes 524288 | tf_op jit(solution)/shard_map/all_to_all | solution.py:69
  38.1 0.3 reshape.279
  38.5 0.5 copy.75
  39.1 2.4 %broadcast_select_fusion.3 = (bf16[16,64,2,64]{3,2,1,0:T(2,128)(2,1)S(1)}, bf16[16,64,2,64]{3,2,1,0:T(2,128)(2,1)}) fusion(bf16[16,64,2,64]{3,2,1,0:T(2,128)(2,1)S(1)} %bitcast.166, pred[16,64]{1,0:T(8,128)(4,1)S(1)} %get-tuple-element.32, bf16[16,2,64]{2,1,0:T(2,128)(2,1)S(1)} %copy.70, bf16[16,64,2,64]{3,2,1,0:T(2,128)(2,1)S(1)} %bitcast.169, ...), kind=kLoop, calls=%fused_computation.47 | loop fusion | flops 262144 | bytes 1057792 | tf_op jit(solution)/shard_map/jit(_where)/select_n | solution.py:49
  41.5 1.1 fusion.54
  42.8 1.6 %convolution_convert_fusion.3 = bf16[16,2,2,64]{3,2,1,0:T(2,128)(2,1)S(1)} fusion(bf16[16,64,2,64]{3,2,1,0:T(2,128)(2,1)} %get-tuple-element.28, f32[16,2,2]{2,1,0:T(2,128)S(1)} %fusion.145, f32[16,2,2,64]{3,2,1,0:T(2,128)S(1)} %fusion.54), kind=kOutput, calls=%fused_computation.41 | convolution fusion | flops 540799 | bytes 286976 | tf_op jit(solution)/shard_map/bgrs,bsgd->bgrd/dot_general | solution.py:55
  44.7 11.9 %psum.28 = bf16[16,1024]{1,0:T(8,128)(2,1)S(1)} all-reduce(bf16[16,1024]{1,0:T(8,128)(2,1)S(1)} %convolution_convert_fusion.1), channel_id=1, replica_groups=mesh['dp'=4,'tp'=4] {'tp'}, use_global_device_ids=true, to_apply=%region_3.4 | all-reduce | flops 16384 | bytes 65536 | tf_op jit(solution)/shard_map/psum | solution.py:56
  56.8 1.0 fusion.104
  58.5 4.6 %fusion.12 = f32[16,32,128]{2,0,1:T(8,128)S(1)} fusion(bf16[2,32,1024,128]{3,2,1,0:T(8,128)(2,1)} %param.31, bf16[16,1024]{1,0:T(8,128)(2,1)S(1)} %fusion.92), kind=kOutput, calls=%fused_computation.12 | convolution fusion | flops 134217728 | bytes 8683520 | tf_op jit(solution)/shard_map/bd,edf->bef/dot_general | solution.py:34
  63.1 7.1 %fusion.47 = bf16[16,1024]{1,0:T(8,128)(2,1)S(1)} fusion(bf16[2,32,128,1024]{3,2,1,0:T(8,128)(2,1)} %param.33, bf16[2,32,1024,128]{3,2,1,0:T(8,128)(2,1)} %param.32, f32[16,32,128]{2,0,1:T(8,128)S(1)} %fusion.12, f32[16,32]{0,1:T(8,128)S(1)} %copy.80, bf16[16,1024]{1,0:T(8,128)(2,1)S(1)} %fusion.92), kind=kOutput, calls=%fused_computation.29 | convolution fusion | flops 268910592 | bytes 17106944 | tf_op jit(solution)/shard_map/bef,efd->bd/dot_general | solution.py:37
  70.2 10.3 %psum.29 = bf16[16,1024]{1,0:T(8,128)(2,1)S(1)} all-reduce(bf16[16,1024]{1,0:T(8,128)(2,1)S(1)} %fusion.47), channel_id=1, replica_groups=mesh['dp'=4,'tp'=4] {'tp'}, use_global_device_ids=true, to_apply=%region_9.10 | all-reduce | flops 16384 | bytes 65536 | tf_op jit(solution)/shard_map/psum | solution.py:58
  80.6 1.2 convolution_convert_fusion.4
  82.5 3.6 %all-to-all-start.3 = ((bf16[4,2,16384]{2,1,0:T(2,128)(2,1)}), bf16[4,2,16384]{2,1,0:T(2,128)(2,1)S(1)}, u32[]{:S(2)}, u32[]{:S(2)}) async-start(bf16[4,2,16384]{2,1,0:T(2,128)(2,1)} %reshape.276), calls=%async_computation.3 | async-start | bytes 524288 | tf_op jit(solution)/shard_map/all_to_all | solution.py:69
  86.7 0.5 copy.87
  87.3 4.4 %all-to-all-done.3 = bf16[4,2,16384]{2,1,0:T(2,128)(2,1)S(1)} async-done(((bf16[4,2,16384]{2,1,0:T(2,128)(2,1)}), bf16[4,2,16384]{2,1,0:T(2,128)(2,1)S(1)}, u32[]{:S(2)}, u32[]{:S(2)}) %all-to-all-start.3) | async-done | bytes 262176 | tf_op jit(solution)/shard_map/all_to_all | solution.py:69
  92.0 0.5 copy.90
  92.6 1.5 %broadcast_select_fusion.1 = (bf16[16,64,2,64]{3,2,1,0:T(2,128)(2,1)S(1)}, bf16[16,64,2,64]{3,2,1,0:T(2,128)(2,1)S(1)}) fusion(bf16[16,64,2,64]{3,2,1,0:T(2,128)(2,1)S(1)} %bitcast.167, pred[16,64]{1,0:T(8,128)(4,1)S(1)} %get-tuple-element.32, bf16[16,2,64]{2,1,0:T(2,128)(2,1)S(1)} %copy.85, bf16[16,64,2,64]{3,2,1,0:T(2,128)(2,1)S(1)} %bitcast.168, ...), kind=kLoop, calls=%fused_computation.45 | loop fusion | flops 262144 | bytes 1057792 | tf_op jit(solution)/shard_map/jit(_where)/select_n | solution.py:49
  94.1 0.4 fusion.55
  94.8 0.5 convolution_convert_fusion.2
  95.5 10.3 %psum.30 = bf16[16,1024]{1,0:T(8,128)(2,1)S(1)} all-reduce(bf16[16,1024]{1,0:T(8,128)(2,1)S(1)} %convolution_convert_fusion), channel_id=1, replica_groups=mesh['dp'=4,'tp'=4] {'tp'}, use_global_device_ids=true, to_apply=%region_13.14 | all-reduce | flops 16384 | bytes 65536 | tf_op jit(solution)/shard_map/psum | solution.py:56
  106.2 4.6 %fusion.6 = f32[16,32,128]{2,0,1:T(8,128)S(1)} fusion(bf16[2,32,1024,128]{3,2,1,0:T(8,128)(2,1)} %param.31, bf16[16,1024]{1,0:T(8,128)(2,1)S(1)} %fusion.100), kind=kOutput, calls=%fused_computation.6 | convolution fusion | flops 134217728 | bytes 8683520 | tf_op jit(solution)/shard_map/bd,edf->bef/dot_general | solution.py:34
  111.5 7.1 %fusion.44 = bf16[16,1024]{1,0:T(8,128)(2,1)S(1)} fusion(bf16[2,32,128,1024]{3,2,1,0:T(8,128)(2,1)} %param.33, bf16[2,32,1024,128]{3,2,1,0:T(8,128)(2,1)} %param.32, f32[16,32,128]{2,0,1:T(8,128)S(1)} %fusion.6, f32[16,32]{0,1:T(8,128)S(1)} %copy.95, bf16[16,1024]{1,0:T(8,128)(2,1)S(1)} %fusion.100), kind=kOutput, calls=%fused_computation.28 | convolution fusion | flops 268910592 | bytes 17106944 | tf_op jit(solution)/shard_map/bef,efd->bd/dot_general | solution.py:37
  118.6 10.3 %psum.31 = bf16[16,1024]{1,0:T(8,128)(2,1)S(1)} all-reduce(bf16[16,1024]{1,0:T(8,128)(2,1)S(1)} %fusion.44), channel_id=1, replica_groups=mesh['dp'=4,'tp'=4] {'tp'}, use_global_device_ids=true, to_apply=%region_19.20 | all-reduce | flops 16384 | bytes 65536 | tf_op jit(solution)/shard_map/psum | solution.py:58
  128.9 0.6 fusion.101
  (70 shorter events, 6.6 us)
Async XLA Ops:
  0.6 55.9 %copy-start = (bf16[16,1024]{1,0:T(8,128)(2,1)S(1)}, bf16[16,1024]{1,0:T(8,128)(2,1)}, u32[]{:S(2)}) copy-start(bf16[16,1024]{1,0:T(8,128)(2,1)} %param.17) | copy-start | bytes 98308
  0.6 43.9 %copy-start.1 = (bf16[2,256,1024]{2,1,0:T(8,128)(2,1)S(1)}, bf16[2,256,1024]{2,1,0:T(8,128)(2,1)}, u32[]{:S(2)}) copy-start(bf16[2,256,1024]{2,1,0:T(8,128)(2,1)} %param.28) | copy-start | bytes 3145732
  3.0 22.6 %all-to-all-start = ((bf16[4,2,16384]{2,1,0:T(2,128)(2,1)}), bf16[4,2,16384]{2,1,0:T(2,128)(2,1)S(1)}, u32[]{:S(2)}, u32[]{:S(2)}) async-start(bf16[4,2,16384]{2,1,0:T(2,128)(2,1)} %reshape.280), calls=%async_computation | async-start | bytes 524288 | tf_op jit(solution)/shard_map/all_to_all | solution.py:69
  25.5 9.2 %all-to-all-start.1 = ((bf16[4,2,16384]{2,1,0:T(2,128)(2,1)}), bf16[4,2,16384]{2,1,0:T(2,128)(2,1)S(1)}, u32[]{:S(2)}, u32[]{:S(2)}) async-start(bf16[4,2,16384]{2,1,0:T(2,128)(2,1)} %reshape.278), calls=%async_computation.1 | async-start | bytes 524288 | tf_op jit(solution)/shard_map/all_to_all | solution.py:69
  34.7 47.7 %all-to-all-start.2 = ((bf16[4,2,16384]{2,1,0:T(2,128)(2,1)}), bf16[4,2,16384]{2,1,0:T(2,128)(2,1)S(1)}, u32[]{:S(2)}, u32[]{:S(2)}) async-start(bf16[4,2,16384]{2,1,0:T(2,128)(2,1)} %reshape.282), calls=%async_computation.2 | async-start | bytes 524288 | tf_op jit(solution)/shard_map/all_to_all | solution.py:69
  41.5 45.8 %copy-start.2 = (bf16[16,64,2,64]{3,2,1,0:T(2,128)(2,1)}, bf16[16,64,2,64]{3,2,1,0:T(2,128)(2,1)S(1)}, u32[]{:S(2)}) copy-start(bf16[16,64,2,64]{3,2,1,0:T(2,128)(2,1)S(1)} %get-tuple-element.27) | copy-start | bytes 786436
  58.5 35.6 %copy-start.6 = (pred[16,64]{1,0:T(8,128)(4,1)S(1)}, pred[16,64]{1,0:T(8,128)(4,1)}, u32[]{:S(2)}) copy-start(pred[16,64]{1,0:T(8,128)(4,1)} %get-tuple-element.31) | copy-start | bytes 3076
  63.1 42.9 %copy-start.5 = (bf16[2,1024,32]{1,2,0:T(8,128)(2,1)S(1)}, bf16[2,1024,32]{1,2,0:T(8,128)(2,1)}, u32[]{:S(2)}) copy-start(bf16[2,1024,32]{1,2,0:T(8,128)(2,1)} %param.30) | copy-start | bytes 393220
  82.5 9.2 %all-to-all-start.3 = ((bf16[4,2,16384]{2,1,0:T(2,128)(2,1)}), bf16[4,2,16384]{2,1,0:T(2,128)(2,1)S(1)}, u32[]{:S(2)}, u32[]{:S(2)}) async-start(bf16[4,2,16384]{2,1,0:T(2,128)(2,1)} %reshape.276), calls=%async_computation.3 | async-start | bytes 524288 | tf_op jit(solution)/shard_map/all_to_all | solution.py:69
  94.1 35.4 %copy-start.3 = (bf16[16,64,2,64]{3,2,1,0:T(2,128)(2,1)}, bf16[16,64,2,64]{3,2,1,0:T(2,128)(2,1)S(1)}, u32[]{:S(2)}) copy-start(bf16[16,64,2,64]{3,2,1,0:T(2,128)(2,1)S(1)} %get-tuple-element.25) | copy-start | bytes 786436
  94.1 35.4 %copy-start.4 = (bf16[16,64,2,64]{3,2,1,0:T(2,128)(2,1)}, bf16[16,64,2,64]{3,2,1,0:T(2,128)(2,1)S(1)}, u32[]{:S(2)}) copy-start(bf16[16,64,2,64]{3,2,1,0:T(2,128)(2,1)S(1)} %get-tuple-element.26) | copy-start | bytes 786436
where the time goes:
time: 131 us; the launch traced here: 130 us
  blocking collectives  42.7 us (33%)
  matrix products  33.4 us (25%)
  local copies, waits for them, and re-layouts  17.6 us (13%)
  starting transfers between devices  14.9 us (11%)
  other arithmetic  12 us (9%)
  waiting for transfers between devices  7.97 us (6%)
    psum x2, blocking collectives, decode_layer(): lax.psum(jnp.dot(attn_vec, w_o, preferred_element_type=jnp.float32).astyp...  22.1 us
    psum x2, blocking collectives, decode_layer(): lax.psum(expert_block(x_mid, choice, g_mlp, w_router, w_gate, w_up, w_dow...  20.5 us
    all_to_all x4, starting transfers between devices, local_step(): lax.all_to_all(cache_blk, 'tp', 2, 1, tiled=True)  14.9 us
    dot_general x2, matrix products, expert_block(): jnp.einsum('bef,efd->bd', expert_in, w_down, preferred_element_type=jnp.f...  14.2 us
    unnamed x26, local copies, waits for them, and re-layouts  10.3 us
    dot_general x2, matrix products, expert_block(): jnp.einsum('bd,edf->bef', normed, w_gate, preferred_element_type=jnp.floa...  9.17 us
    all_to_all x4, waiting for transfers between devices, local_step(): lax.all_to_all(cache_blk, 'tp', 2, 1, tiled=True)  7.97 us
    select_n x2, other arithmetic, decode_layer(): key_cache = jnp.where(is_new, key_new[:, None], key_cache)  3.9 us
  transfers between devices with their start and end apart: 4, of which 2 were waited for; matrix products, arithmetic and copies ran while one was open for 34% of the time, Pallas kernels for 0%

commit v1 on v0

v1 whole, which is shorter than its diff:
```python
import math

import jax
import jax.numpy as jnp
from jax import lax
from jax.experimental import pallas as pl
from jax.experimental.pallas import tpu as pltpu
from jax.sharding import PartitionSpec as P

EPS = 1e-5
THETA = 1000000.0
LAYERS = 2
B = 16
SEQ = 64
D = 1024
HEAD = 64
EXPERTS = 32
TP = 4
LOCAL = SEQ // TP
CHUNKS = 4
CB = B // CHUNKS
WCH = 8
EPC = EXPERTS // WCH
NCH = 4
NW = D // NCH
BF = jnp.bfloat16
F32 = jnp.float32
MESH = pl.DeviceIdType.MESH
NT = (((1,), (1,)), ((), ()))


def dot(a, b):
    return jnp.dot(a, b, preferred_element_type=F32)


def dot_nt(a, b):
    return lax.dot_general(a, b, NT, preferred_element_type=F32)


def iota(shape, dim):
    return lax.broadcasted_iota(jnp.int32, shape, dim)


def kernel(lens, hid, cho, k1, v1, k2, v2, ga, wq, wk, wv, wo, gm, wr, wg, wu, wd,
           h_out, ko1, vo1, ko2, vo2,
           lens_s, hid_b, cho_b, ga_b, gm_b, wq_b, wk_b, wv_b, wo_b, wr_b, wg_b, wu_b, wd_b,
           kin, stage, send, recv, istage, kst, vst, kvn, ar, ub, hst,
           sm, cs, ws, es, ss, rs, ass, ars, osem):
    me = lax.axis_index('tp')
    peers = {1: me + 1 - 2 * (me % 2), 2: (me + 2) % 4, 3: 3 - me}
    caches = ((k1, v1), (k2, v2))
    outs = ((ko1, vo1), (ko2, vo2))

    def cache_in(l, kv, c):
        sl = pl.ds(c * CB, CB)
        return pltpu.make_async_copy(caches[l][kv].at[sl], kin.at[l, kv, sl], cs.at[l, kv, c])

    smalls = [pltpu.make_async_copy(s, d, sm.at[i]) for i, (s, d) in enumerate(
        ((lens, lens_s), (hid, hid_b), (cho, cho_b), (ga, ga_b), (gm, gm_b), (wr, wr_b)))]

    def proj_in(l):
        return [pltpu.make_async_copy(s.at[l], d.at[l], ws.at[l, i]) for i, (s, d) in enumerate(
            ((wq, wq_b), (wk, wk_b), (wv, wv_b), (wo, wo_b)))]

    def expert_in(l, c):
        sl = pl.ds(c * EPC, EPC)
        rl = pl.ds(c * EPC * 128, EPC * 128)
        return [pltpu.make_async_copy(wg.at[l, sl], wg_b.at[l, sl], es.at[l, 0, c]),
                pltpu.make_async_copy(wu.at[l, sl], wu_b.at[l, sl], es.at[l, 1, c]),
                pltpu.make_async_copy(wd.at[l, rl], wd_b.at[l, rl], es.at[l, 2, c])]

    for c in range(CHUNKS):
        for kv in range(2):
            cache_in(0, kv, c).start()
    for cp in smalls + proj_in(0):
        cp.start()
    bar = pltpu.get_barrier_semaphore()
    for j in (1, 2, 3):
        pl.semaphore_signal(bar, inc=1, device_id={'tp': peers[j]}, device_id_type=MESH)
    for c in range(CHUNKS):
        for kv in range(2):
            cache_in(1, kv, c).start()
    for l in range(LAYERS):
        for c in range(WCH):
            for cp in expert_in(l, c):
                cp.start()
        if l == 0:
            for cp in proj_in(1):
                cp.start()
    pl.semaphore_wait(bar, 3)

    def kv_send(l, c, j):
        sl = pl.ds(c * CB, CB)
        return pltpu.make_async_remote_copy(
            send.at[l, peers[j], sl], recv.at[l, sl, me], ss.at[l, c, j - 1], rs.at[l, c, j - 1],
            device_id={'tp': peers[j]}, device_id_type=MESH)

    def kv_recv(l, c, j):
        sl = pl.ds(c * CB, CB)
        return pltpu.make_async_remote_copy(
            send.at[l, me, sl], recv.at[l, sl, peers[j]], ss.at[l, c, j - 1], rs.at[l, c, j - 1],
            device_id={'tp': peers[j]}, device_id_type=MESH)

    def pack_send(l):
        for c in range(CHUNKS):
            for kv in range(2):
                cache_in(l, kv, c).wait()
            sl = pl.ds(c * CB, CB)
            kf = kin[l, 0, sl].astype(F32).reshape(CB * LOCAL * 8, HEAD)
            vf = kin[l, 1, sl].astype(F32).reshape(CB * LOCAL * 8, HEAD)
            stage[...] = jnp.concatenate([kf, vf], axis=1)
            for h in range(8):
                rows = stage[pl.ds(h, CB * LOCAL, stride=8), :].astype(BF)
                send[l, h // 2, sl, h % 2] = rows.reshape(CB, LOCAL, 128)
            recv[l, sl, me] = send[l, me, sl]
            for j in (2, 3, 1):
                kv_send(l, c, j).start()

    def ar_copy(a, n, j, slot):
        return pltpu.make_async_remote_copy(
            ar.at[a, me, n], ar.at[a, slot, n], ass.at[a, n, j - 1], ars.at[a, n, j - 1],
            device_id={'tp': peers[j]}, device_id_type=MESH)

    def ar_send(a, n, value):
        ar[a, me, n] = value.astype(BF)
        for j in (2, 3, 1):
            ar_copy(a, n, j, me).start()

    def ar_sum(a, h):
        parts = []
        for n in range(NCH):
            for j in (1, 2, 3):
                ar_copy(a, n, j, peers[j]).wait_recv()
            tot = ar[a, 0, n].astype(F32)
            for s in range(1, TP):
                tot = tot + ar[a, s, n].astype(F32)
            parts.append(tot)
        return (h.astype(F32) + jnp.concatenate(parts, axis=1)).astype(BF)

    def rms(h, gain):
        hf = h.astype(F32)
        scale = lax.rsqrt(jnp.mean(hf * hf, axis=1, keepdims=True) + EPS)
        return (hf * scale * gain.astype(F32)).astype(BF)

    lane = iota((B, 128), 1)
    low = lane < HEAD

    def rope(x, cosv, sinv):
        rot = jnp.where((lane % HEAD) < HEAD // 2, pltpu.roll(x, 128 - HEAD // 2, 1), pltpu.roll(x, HEAD // 2, 1))
        return (x * cosv + rot * sinv).astype(BF).astype(F32)

    pack_send(0)
    for cp in smalls:
        cp.wait()
    lenv = jnp.zeros((B, 128), jnp.int32)
    rowi = iota((B, 128), 0)
    for b in range(B):
        lenv = jnp.where(rowi == b, lens_s[b], lenv)
    freq = jnp.exp((lane % (HEAD // 2)).astype(F32) * (-2.0 * math.log(THETA) / HEAD))
    ang = lenv.astype(F32) * freq
    cosv = jnp.cos(ang)
    sinv = jnp.sin(ang)
    sinv = jnp.where((lane % HEAD) < HEAD // 2, -sinv, sinv)

    row64 = iota((64, 128), 0)
    rowb = row64 % B
    col = iota((64, 128), 1)
    pos = (col // 32) * LOCAL + col % LOCAL
    same = ((col // LOCAL) % 2) == (row64 // 32)
    len64 = jnp.concatenate([lenv] * 4, axis=0)
    valid = same & (pos <= len64)
    isnew = same & (pos == len64)

    def attention(l, h):
        a = rms(h, ga_b[l:l + 1, :])
        for cp in proj_in(l):
            cp.wait()
        q = dot(a, wq_b[l])
        k = rope(dot(a, wk_b[l]), cosv, sinv)
        v = dot(a, wv_b[l]).astype(BF).astype(F32)
        new0 = jnp.where(low, k, pltpu.roll(v, HEAD, 1))
        new1 = jnp.where(low, pltpu.roll(k, HEAD, 1), v)
        kvn[l, 0] = new0
        kvn[l, 1] = new1
        qs = []
        for i in range(2):
            qi = rope(q[:, i * 128:(i + 1) * 128], cosv, sinv)
            qs.append(jnp.where(low, qi, 0.0))
            qs.append(jnp.where(low, pltpu.roll(qi, HEAD, 1), 0.0))
        qf = jnp.concatenate(qs, axis=0)
        newr = jnp.concatenate([new0, new0, new1, new1], axis=0)
        qb = qf.astype(BF)
        snew = jnp.sum(qf * newr, axis=1, keepdims=True)
        s = jnp.zeros((64, 128), F32)
        for c in range(CHUNKS):
            for j in (1, 2, 3):
                kv_recv(l, c, j).wait_recv()
            for b in range(c * CB, (c + 1) * CB, 2):
                kvb = recv[l, b:b + 2].reshape(256, 128)
                sb = dot_nt(qb, kvb)
                s = jnp.where(rowb == b, sb[:, :128], s)
                s = jnp.where(rowb == b + 1, sb[:, 128:], s)
        s = jnp.where(isnew, snew, s) * (HEAD ** -0.5)
        s = jnp.where(valid, s, -1e30)
        e = jnp.exp(s - jnp.max(s, axis=1, keepdims=True))
        p = (e / jnp.sum(e, axis=1, keepdims=True)).astype(BF).astype(F32)
        pn = jnp.sum(jnp.where(isnew, p, 0.0), axis=1, keepdims=True)
        p = jnp.where(isnew, 0.0, p)
        o = pn * newr
        for b in range(0, B, 2):
            pb = jnp.concatenate([jnp.where(rowb == b, p, 0.0), jnp.where(rowb == b + 1, p, 0.0)], axis=1).astype(BF)
            o = o + dot(pb, recv[l, b:b + 2].reshape(256, 128))
        att = jnp.concatenate(
            [jnp.where(low, pltpu.roll(o[32 * i:32 * i + 16], HEAD, 1), o[32 * i + 16:32 * i + 32]) for i in range(2)],
            axis=1).astype(BF)
        for n in range(NCH):
            ar_send(2 * l, n, dot(att, wo_b[l, :, n * NW:(n + 1) * NW]))

    def cache_out(l, kv):
        return pltpu.make_async_copy((kst, vst)[kv].at[l], outs[l][kv], osem.at[l, kv])

    def write_caches(l):
        row = iota((SEQ, 128), 0)

        def body(b, carry):
            kvb = recv[l, b].astype(F32)
            for g in range(2):
                x = kvb[:, g].reshape(SEQ, 128)
                x = jnp.where(row == lens_s[b], kvn[l, g, pl.ds(b, 1), :], x)
                istage[pl.ds(g, SEQ, stride=2), :] = x
            z = istage[...]
            kst[l, b] = z[:, :HEAD].astype(BF)
            vst[l, b] = z[:, HEAD:].astype(BF)
            return carry

        lax.fori_loop(0, B, body, 0)
        for kv in range(2):
            cache_out(l, kv).start()

    def gates(l, m):
        choice = cho_b[l]
        onehot = jnp.zeros((EXPERTS, B), F32)
        erow = iota((EXPERTS, B), 0)
        for j in range(8):
            onehot = onehot + (erow == choice[j:j + 1, :]).astype(F32)
        eye = (iota((B, B), 0) == iota((B, B), 1)).astype(BF)
        mask = dot_nt(eye, onehot.astype(BF)) > 0.5
        logits = jnp.where(mask, dot_nt(m, wr_b[l]), -1e30)
        ex = jnp.where(mask, jnp.exp(logits - jnp.max(logits, axis=1, keepdims=True)), 0.0)
        return ex / jnp.sum(ex, axis=1, keepdims=True)

    def experts(l, h1):
        m = rms(h1, gm_b[l:l + 1, :])
        gate = gates(l, m)
        for c in range(WCH):
            for cp in expert_in(l, c):
                cp.wait()
        for e in range(EXPERTS):
            acc = None
            for kk in range(4):
                ks = slice(kk * 256, (kk + 1) * 256)
                w = jnp.concatenate([wg_b[l, e, ks, :], wu_b[l, e, ks, :]], axis=1)
                t = dot(m[:, ks], w)
                acc = t if acc is None else acc + t
            ga_act, up = acc[:, :128], acc[:, 128:]
            act = ga_act * jax.nn.sigmoid(ga_act) * up * gate[:, e:e + 1]
            ub[:, e * 128:(e + 1) * 128] = act.astype(BF)
        for n in range(NCH):
            ar_send(2 * l + 1, n, dot(ub[...], wd_b[l, :, n * NW:(n + 1) * NW]))

    h = hid_b[...]
    for l in range(LAYERS):
        attention(l, h)
        if l == 0:
            pack_send(1)
        write_caches(l)
        h1 = ar_sum(2 * l, h)
        experts(l, h1)
        h = ar_sum(2 * l + 1, h1)
    hst[...] = h
    hcp = pltpu.make_async_copy(hst, h_out, sm.at[6])
    hcp.start()
    for l in range(LAYERS):
        for c in range(CHUNKS):
            for j in (1, 2, 3):
                kv_send(l, c, j).wait_send()
        for a in (2 * l, 2 * l + 1):
            for n in range(NCH):
                for j in (1, 2, 3):
                    ar_copy(a, n, j, me).wait_send()
        for kv in range(2):
            cache_out(l, kv).wait()
    hcp.wait()


def solution(mesh):
    seq_spec = P('dp', 'tp', None, None)
    head_spec = P('dp', None, 'tp', None)
    col_spec = P(None, None, 'tp')
    ff_spec = P(None, None, None, 'tp')
    anyspec = pl.BlockSpec(memory_space=pl.ANY)
    dma = pltpu.SemaphoreType.DMA

    def local_step(hidden, lengths, choice, keys_one, vals_one, keys_two, vals_two, g_attn, w_q, w_k, w_v, w_o, g_mlp, w_router, w_gate, w_up, w_down):
        cho = jnp.transpose(choice, (0, 2, 1))
        wr = jnp.transpose(w_router, (0, 2, 1))
        wd = w_down.reshape(LAYERS, EXPERTS * 128, D)
        cache_shape = jax.ShapeDtypeStruct((B, SEQ * 2, HEAD), BF)
        h, k1, v1, k2, v2 = pl.pallas_call(
            kernel,
            out_shape=(jax.ShapeDtypeStruct((B, D), BF),) + (cache_shape,) * 4,
            in_specs=[anyspec] * 17,
            out_specs=(anyspec,) * 5,
            scratch_shapes=[
                pltpu.SMEM((B,), jnp.int32),
                pltpu.VMEM((B, D), BF),
                pltpu.VMEM((LAYERS, 8, B), jnp.int32),
                pltpu.VMEM((LAYERS, D), BF),
                pltpu.VMEM((LAYERS, D), BF),
                pltpu.VMEM((LAYERS, D, 256), BF),
                pltpu.VMEM((LAYERS, D, 128), BF),
                pltpu.VMEM((LAYERS, D, 128), BF),
                pltpu.VMEM((LAYERS, 256, D), BF),
                pltpu.VMEM((LAYERS, EXPERTS, D), BF),
                pltpu.VMEM((LAYERS, EXPERTS, D, 128), BF),
                pltpu.VMEM((LAYERS, EXPERTS, D, 128), BF),
                pltpu.VMEM((LAYERS, EXPERTS * 128, D), BF),
                pltpu.VMEM((LAYERS, 2, B, LOCAL, 8, HEAD), BF),
                pltpu.VMEM((CB * LOCAL * 8, 128), F32),
                pltpu.VMEM((LAYERS, TP, B, 2, LOCAL, 128), BF),
                pltpu.VMEM((LAYERS, B, TP, 2, LOCAL, 128), BF),
                pltpu.VMEM((2 * SEQ, 128), F32),
                pltpu.VMEM((LAYERS, B, 2 * SEQ, HEAD), BF),
                pltpu.VMEM((LAYERS, B, 2 * SEQ, HEAD), BF),
                pltpu.VMEM((LAYERS, 2, B, 128), F32),
                pltpu.VMEM((2 * LAYERS, TP, NCH, B, NW), BF),
                pltpu.VMEM((B, EXPERTS * 128), BF),
                pltpu.VMEM((B, D), BF),
                dma((7,)),
                dma((LAYERS, 2, CHUNKS)),
                dma((LAYERS, 4)),
                dma((LAYERS, 3, WCH)),
                dma((LAYERS, CHUNKS, 3)),
                dma((LAYERS, CHUNKS, 3)),
                dma((2 * LAYERS, NCH, 3)),
                dma((2 * LAYERS, NCH, 3)),
                dma((LAYERS, 2)),
            ],
            compiler_params=pltpu.CompilerParams(collective_id=0, has_side_effects=True, vmem_limit_bytes=67_000_000),
            name='decode_two_layers',
        )(lengths, hidden, cho, keys_one, vals_one, keys_two, vals_two, g_attn, w_q, w_k, w_v, w_o, g_mlp, wr, w_gate, w_up, wd)
        shape = (B, SEQ, 2, HEAD)
        return (h, k1.reshape(shape), v1.reshape(shape), k2.reshape(shape), v2.reshape(shape))

    return jax.shard_map(local_step, mesh=mesh, in_specs=(P('dp', None), P('dp'), P(None, 'dp', None), seq_spec, seq_spec, seq_spec, seq_spec, P(), col_spec, col_spec, col_spec, P(None, 'tp', None), P(), P(), ff_spec, ff_spec, P(None, None, 'tp', None)), out_specs=(P('dp', None), head_spec, head_spec, head_spec, head_spec), check_vma=False)
```

time: 131 us -> 55.3 us (0.42)
  Pallas kernels: 0 us -> 44.1 us
  blocking collectives: 42.7 us -> 0 us
  matrix products: 33.4 us -> 0 us
  starting transfers between devices: 14.9 us -> 0 us
  other arithmetic: 12 us -> 0 us
  waiting for transfers between devices: 7.97 us -> 0 us
  local copies, waits for them, and re-layouts: 17.6 us -> 10.3 us
    pallas_call x0 -> x1, Pallas kernels: none -> 44.1 us  [local_step(): pl.pallas_call(kernel, out_shape=(jax.ShapeDtypeStruct((B, D), BF),) + (c...]
    psum x4 -> x0, blocking collectives: 42.7 us -> none  [the longest x2 22.1 us: decode_layer(): lax.psum(jnp.dot(attn_vec, w_o, preferred_element_type=jnp.float32).astyp...]
    dot_general x18 -> x0, matrix products: 33.4 us -> none  [the longest x2 14.2 us: expert_block(): jnp.einsum('bef,efd->bd', expert_in, w_down, preferred_element_type=jnp.f...]
    all_to_all x4 -> x0, starting transfers between devices: 14.9 us -> none  [local_step(): lax.all_to_all(cache_blk, 'tp', 2, 1, tiled=True)]
    all_to_all x4 -> x0, waiting for transfers between devices: 7.97 us -> none  [local_step(): lax.all_to_all(cache_blk, 'tp', 2, 1, tiled=True)]
    select_n x2 -> x0, other arithmetic: 3.9 us -> none  [decode_layer(): key_cache = jnp.where(is_new, key_new[:, None], key_cache)]
    dot_general x6 -> x0, local copies, waits for them, and re-layouts: 3.04 us -> none  [the longest x3 1.68 us: decode_layer(): jnp.dot(normed, w_q, preferred_element_type=jnp.float32)]
    reduce_sum x10 -> x0, other arithmetic: 2.21 us -> none  [the longest x4 1.26 us: rms_norm(): jnp.mean(tensor_f * tensor_f, axis=-1, keepdims=True) + EPS]
  transfers between devices with their start and end apart: 4 -> 0, of which waited for: 2 -> 0; matrix products, arithmetic and copies ran while one was open for 34% -> 0% of each run, Pallas kernels for 0% -> 0%
where the time goes in v1:
time: 55.3 us; the launch traced here: 55 us
  Pallas kernels  44.1 us (80%)
  local copies, waits for them, and re-layouts  10.3 us (19%)
  between operations  0.65 us (1%)
    pallas_call x1, Pallas kernels, local_step(): pl.pallas_call(kernel, out_shape=(jax.ShapeDtypeStruct((B, D), BF),) + (c...  44.1 us
    unnamed x5, local copies, waits for them, and re-layouts  10.3 us

profile of v1, /device:TPU:0, one launch (start us, length us, event | category | flops | bytes accessed | tf_op | source)
XLA Modules:
  0.0 55.0 jit_solution(1169040737926481801)
XLA Ops:
  0.6 44.1 %decode_two_layers.1 = (bf16[16,1024]{1,0:T(8,128)(2,1)}, bf16[16,128,64]{2,1,0:T(8,128)(2,1)}, bf16[16,128,64]{2,1,0:T(8,128)(2,1)}, bf16[16,128,64]{2,1,0:T(8,128)(2,1)}, bf16[16,128,64]{2,1,0:T(8,128)(2,1)}) custom-call(s32[16]{0:T(128)} %lens.1, bf16[16,1024]{1,0:T(8,128)(2,1)} %hid.1, s32[2,8,16]{2,1,0:T(8,128)} %bitcast.13, ...), custom_call_target="tpu_custom_call" | custom-call | tf_op jit(solution)/shard_map/decode_two_layers/pallas_call | solution.py:309
  44.7 1.4 %copy.27 = bf16[16,1024]{1,0:T(8,128)(2,1)} copy(bf16[16,1024]{1,0:T(8,128)(2,1)} %get-tuple-element.20) | data formatting | bytes 65536
  46.1 2.2 %copy.28 = bf16[16,64,2,64]{3,2,1,0:T(2,128)(2,1)} copy(bf16[16,64,2,64]{3,2,1,0:T(2,128)(2,1)} %bitcast.11) | data formatting | bytes 524288
  48.3 2.2 %copy.29 = bf16[16,64,2,64]{3,2,1,0:T(2,128)(2,1)} copy(bf16[16,64,2,64]{3,2,1,0:T(2,128)(2,1)} %bitcast.10) | data formatting | bytes 524288
  50.5 2.2 %copy.30 = bf16[16,64,2,64]{3,2,1,0:T(2,128)(2,1)} copy(bf16[16,64,2,64]{3,2,1,0:T(2,128)(2,1)} %bitcast.9) | data formatting | bytes 524288
  52.8 2.2 %copy.31 = bf16[16,64,2,64]{3,2,1,0:T(2,128)(2,1)} copy(bf16[16,64,2,64]{3,2,1,0:T(2,128)(2,1)} %bitcast.8) | data formatting | bytes 524288

commit v2 on v1

--- a/solution.py
+++ b/solution.py
@@ -42,10 +42,10 @@
 
 
 def kernel(lens, hid, cho, k1, v1, k2, v2, ga, wq, wk, wv, wo, gm, wr, wg, wu, wd,
-           h_out, ko1, vo1, ko2, vo2,
+           hst, ko1, vo1, ko2, vo2,
            lens_s, hid_b, cho_b, ga_b, gm_b, wq_b, wk_b, wv_b, wo_b, wr_b, wg_b, wu_b, wd_b,
-           kin, stage, send, recv, istage, kst, vst, kvn, ar, ub, hst,
-           sm, cs, ws, es, ss, rs, ass, ars, osem):
+           kin, stage, send, recv, istage, kvn, ar, ub,
+           sm, cs, ws, es, ss, rs, ass, ars):
     me = lax.axis_index('tp')
     peers = {1: me + 1 - 2 * (me % 2), 2: (me + 2) % 4, 3: 3 - me}
     caches = ((k1, v1), (k2, v2))
@@ -216,9 +216,6 @@
         for n in range(NCH):
             ar_send(2 * l, n, dot(att, wo_b[l, :, n * NW:(n + 1) * NW]))
 
-    def cache_out(l, kv):
-        return pltpu.make_async_copy((kst, vst)[kv].at[l], outs[l][kv], osem.at[l, kv])
-
     def write_caches(l):
         row = iota((SEQ, 128), 0)
 
@@ -229,13 +226,11 @@
                 x = jnp.where(row == lens_s[b], kvn[l, g, pl.ds(b, 1), :], x)
                 istage[pl.ds(g, SEQ, stride=2), :] = x
             z = istage[...]
-            kst[l, b] = z[:, :HEAD].astype(BF)
-            vst[l, b] = z[:, HEAD:].astype(BF)
+            outs[l][0][b] = z[:, :HEAD].astype(BF)
+            outs[l][1][b] = z[:, HEAD:].astype(BF)
             return carry
 
         lax.fori_loop(0, B, body, 0)
-        for kv in range(2):
-            cache_out(l, kv).start()
 
     def gates(l, m):
         choice = cho_b[l]
@@ -278,8 +273,6 @@
         experts(l, h1)
         h = ar_sum(2 * l + 1, h1)
     hst[...] = h
-    hcp = pltpu.make_async_copy(hst, h_out, sm.at[6])
-    hcp.start()
     for l in range(LAYERS):
         for c in range(CHUNKS):
             for j in (1, 2, 3):
@@ -288,9 +281,15 @@
             for n in range(NCH):
                 for j in (1, 2, 3):
                     ar_copy(a, n, j, me).wait_send()
-        for kv in range(2):
-            cache_out(l, kv).wait()
-    hcp.wait()
+
+
+def write_out(*refs):
+    srcs, dsts, sem = refs[:5], refs[5:10], refs[10]
+    copies = [pltpu.make_async_copy(s, d, sem.at[i]) for i, (s, d) in enumerate(zip(srcs, dsts))]
+    for cp in copies:
+        cp.start()
+    for cp in copies:
+        cp.wait()
 
 
 def solution(mesh):
@@ -305,12 +304,12 @@
         cho = jnp.transpose(choice, (0, 2, 1))
         wr = jnp.transpose(w_router, (0, 2, 1))
         wd = w_down.reshape(LAYERS, EXPERTS * 128, D)
-        cache_shape = jax.ShapeDtypeStruct((B, SEQ * 2, HEAD), BF)
-        h, k1, v1, k2, v2 = pl.pallas_call(
+        shapes = ((B, D),) + ((B, SEQ * 2, HEAD),) * 4
+        results = pl.pallas_call(
             kernel,
-            out_shape=(jax.ShapeDtypeStruct((B, D), BF),) + (cache_shape,) * 4,
+            out_shape=tuple(pltpu.VMEM(s, BF) for s in shapes),
             in_specs=[anyspec] * 17,
-            out_specs=(anyspec,) * 5,
+            out_specs=(pl.BlockSpec(memory_space=pltpu.VMEM),) * 5,
             scratch_shapes=[
                 pltpu.SMEM((B,), jnp.int32),
                 pltpu.VMEM((B, D), BF),
@@ -330,13 +329,10 @@
                 pltpu.VMEM((LAYERS, TP, B, 2, LOCAL, 128), BF),
                 pltpu.VMEM((LAYERS, B, TP, 2, LOCAL, 128), BF),
                 pltpu.VMEM((2 * SEQ, 128), F32),
-                pltpu.VMEM((LAYERS, B, 2 * SEQ, HEAD), BF),
-                pltpu.VMEM((LAYERS, B, 2 * SEQ, HEAD), BF),
                 pltpu.VMEM((LAYERS, 2, B, 128), F32),
                 pltpu.VMEM((2 * LAYERS, TP, NCH, B, NW), BF),
                 pltpu.VMEM((B, EXPERTS * 128), BF),
-                pltpu.VMEM((B, D), BF),
-                dma((7,)),
+                dma((6,)),
                 dma((LAYERS, 2, CHUNKS)),
                 dma((LAYERS, 4)),
                 dma((LAYERS, 3, WCH)),
@@ -344,11 +340,19 @@
                 dma((LAYERS, CHUNKS, 3)),
                 dma((2 * LAYERS, NCH, 3)),
                 dma((2 * LAYERS, NCH, 3)),
-                dma((LAYERS, 2)),
             ],
-            compiler_params=pltpu.CompilerParams(collective_id=0, has_side_effects=True, vmem_limit_bytes=67_000_000),
+            compiler_params=pltpu.CompilerParams(collective_id=0, has_side_effects=True, vmem_limit_bytes=63_500_000),
             name='decode_two_layers',
         )(lengths, hidden, cho, keys_one, vals_one, keys_two, vals_two, g_attn, w_q, w_k, w_v, w_o, g_mlp, wr, w_gate, w_up, wd)
+        h, k1, v1, k2, v2 = pl.pallas_call(
+            write_out,
+            out_shape=tuple(jax.ShapeDtypeStruct(s, BF) for s in shapes),
+            in_specs=[pl.BlockSpec(memory_space=pltpu.VMEM)] * 5,
+            out_specs=(anyspec,) * 5,
+            scratch_shapes=[dma((5,))],
+            compiler_params=pltpu.CompilerParams(vmem_limit_bytes=1_000_000),
+            name='write_out',
+        )(*results)
         shape = (B, SEQ, 2, HEAD)
         return (h, k1.reshape(shape), v1.reshape(shape), k2.reshape(shape), v2.reshape(shape))
 

time: 55.3 us -> 45.7 us (0.83)
  local copies, waits for them, and re-layouts: 10.3 us -> 0 us
  Pallas kernels: 44.1 us -> 44.9 us
    unnamed x5 -> x0, local copies, waits for them, and re-layouts: 10.3 us -> none
    pallas_call x1 -> x2, Pallas kernels: 44.1 us -> 44.9 us  [the longest x1 43.5 us: local_step(): pl.pallas_call(kernel, out_shape=tuple((pltpu.VMEM(s, BF) for s in shapes...]
where the time goes in v2:
time: 45.7 us; the launch traced here: 45.5 us
  Pallas kernels  44.9 us (98%)
  between operations  0.65 us (1%)
    pallas_call x1, Pallas kernels, local_step(): pl.pallas_call(kernel, out_shape=tuple((pltpu.VMEM(s, BF) for s in shapes...  43.5 us
    pallas_call x1, Pallas kernels, local_step(): pl.pallas_call(write_out, out_shape=tuple((jax.ShapeDtypeStruct(s, BF) fo...  1.37 us

profile of v2, /device:TPU:0, one launch (start us, length us, event | category | flops | bytes accessed | tf_op | source)
XLA Modules:
  0.0 45.5 jit_solution(16888718584856224103)
XLA Ops:
  0.6 43.5 %decode_two_layers.1 = (bf16[16,1024]{1,0:T(8,128)(2,1)S(1)}, bf16[16,128,64]{2,1,0:T(8,128)(2,1)S(1)}, bf16[16,128,64]{2,1,0:T(8,128)(2,1)S(1)}, bf16[16,128,64...) custom-call(s32[16]{0:T(128)} %lens.1, bf16[16,1024]{1,0:T(8,128)(2,1)} %hid.1, s32[2,8,16]{2,1,0:T(8,128)} %bitcast.9, ...), custom_call_target="tpu_custom_call" | custom-call | tf_op jit(solution)/shard_map/decode_two_layers/pallas_call | solution.py:308
  44.2 1.4 %write_out.1 = (bf16[16,1024]{1,0:T(8,128)(2,1)}, bf16[16,128,64]{2,1,0:T(8,128)(2,1)}, bf16[16,128,64]{2,1,0:T(8,128)(2,1)}, bf16[16,128,64]{2,1,0:T(8,128)(2,1)}, bf16[16,128,64]{2,1,0:T(8,128)(2,1)}) custom-call(bf16[16,1024]{1,0:T(8,128)(2,1)S(1)} %get-tuple-element.15.refs_0_, bf16[16,128,64]{2,1,0:T(8,128)(2,1)S(1)} %get-tuple-element.16.refs_1_, ...), custom_call_target="tpu_custom_call" | custom-call | tf_op jit(solution)/shard_map/write_out/pallas_call | solution.py:347

commit v3 on v2

v3 whole, which is shorter than its diff:
```python
import math

import jax
import jax.numpy as jnp
from jax import lax
from jax.experimental import pallas as pl
from jax.experimental.pallas import tpu as pltpu
from jax.sharding import PartitionSpec as P

EPS = 1e-5
THETA = 1000000.0
LAYERS = 2
B = 16
SEQ = 64
D = 1024
HEAD = 64
EXPERTS = 32
TP = 4
LOCAL = SEQ // TP
CHUNKS = 4
CB = B // CHUNKS
WCH = 8
EPC = EXPERTS // WCH
NCH = 4
NW = D // NCH
BF = jnp.bfloat16
F32 = jnp.float32
MESH = pl.DeviceIdType.MESH
NT = (((1,), (1,)), ((), ()))


def dot(a, b):
    return jnp.dot(a, b, preferred_element_type=F32)


def dot_nt(a, b):
    return lax.dot_general(a, b, NT, preferred_element_type=F32)


def iota(shape, dim):
    return lax.broadcasted_iota(jnp.int32, shape, dim)


def kernel(lens, hid, cho, k1, v1, k2, v2, ga, wq, wk, wv, wo, gm, wr, wg, wu, wd,
           hst, ko1, vo1, ko2, vo2,
           lens_s, hid_b, cho_b, g_b, proj_b, wr_b, exp_b,
           kin, stage, send, recv, istage, kvn, ar, ub,
           sm, cs, ws, es, ss, rs, ass, ars):
    me = lax.axis_index('tp')
    peers = {1: me + 1 - 2 * (me % 2), 2: (me + 2) % 4, 3: 3 - me}
    caches = ((k1, v1), (k2, v2))
    outs = ((ko1, vo1), (ko2, vo2))

    def cache_in(l, kv, c):
        return pltpu.make_async_copy(caches[l][kv].at[pl.ds(c * CB, CB)], kin.at[l, c, kv], cs.at[c if l == 0 else CHUNKS])

    def all_of(ref, sem):
        return pltpu.make_async_copy(ref, ref, sem)

    smalls = [pltpu.make_async_copy(s, d, sm.at[min(i, 4)]) for i, (s, d) in enumerate(
        ((lens, lens_s), (hid, hid_b), (cho, cho_b), (wr, wr_b), (ga, g_b.at[0]), (gm, g_b.at[1])))]

    def proj_in(l):
        cols = [pl.ds(i * 128, 128) for i in range(8)]
        pairs = [(wk.at[l], proj_b.at[l, 2]), (wv.at[l], proj_b.at[l, 3])]
        pairs += [(wq.at[l, :, cols[i]], proj_b.at[l, i]) for i in range(2)]
        pairs += [(wo.at[l, :, cols[i]], proj_b.at[l, 4 + i // 4, pl.ds(i % 4 * 256, 256)]) for i in range(8)]
        return [pltpu.make_async_copy(s, d, ws.at[l]) for s, d in pairs]

    def proj_wait(l):
        all_of(proj_b.at[l], ws.at[l]).wait()

    def wo_col(l, i):
        return proj_b[l, 4 + i // 4, i % 4 * 256:(i % 4 + 1) * 256, :]

    def expert_in(l, c):
        rows = EPC * D
        sl = pl.ds(c * rows, rows)
        down = exp_b.at[l, 2, pl.ds(c * EXPERTS * 128, EXPERTS * 128)]
        return [pltpu.make_async_copy(wg.at[l, sl], exp_b.at[l, 0, sl], es.at[l]),
                pltpu.make_async_copy(wu.at[l, sl], exp_b.at[l, 1, sl], es.at[l]),
                pltpu.make_async_copy(wd.at[l, :, pl.ds(c * 128, 128)], down, es.at[l])]

    def expert_wait(l):
        all_of(exp_b.at[l], es.at[l]).wait()

    for c in range(CHUNKS):
        for kv in range(2):
            cache_in(0, kv, c).start()
    for cp in smalls + proj_in(0):
        cp.start()
    bar = pltpu.get_barrier_semaphore()
    for j in (1, 2, 3):
        pl.semaphore_signal(bar, inc=1, device_id={'tp': peers[j]}, device_id_type=MESH)
    for c in range(CHUNKS):
        for kv in range(2):
            cache_in(1, kv, c).start()
    with jax.named_scope('barrier'):
        pl.semaphore_wait(bar, 3)

    def kv_send(l, c, j):
        sl = pl.ds(c * CB, CB)
        return pltpu.make_async_remote_copy(
            send.at[l, peers[j], sl], recv.at[l, sl, me], ss, rs.at[c if l == 0 else CHUNKS],
            device_id={'tp': peers[j]}, device_id_type=MESH)

    def kv_wait(l, c, n):
        all_of(recv.at[l, pl.ds(c * CB, n * CB), pl.ds(0, 3)], rs.at[c if l == 0 else CHUNKS]).wait()

    def start_sends(l, c):
        for j in (2, 3, 1):
            kv_send(l, c, j).start()

    def pack(l):
        for c in range(CHUNKS):
            if l == 0:
                all_of(kin.at[l, c], cs.at[c]).wait()
            elif c == 0:
                all_of(kin.at[l], cs.at[CHUNKS]).wait()
            sl = pl.ds(c * CB, CB)
            kf = kin[l, c, 0].astype(F32).reshape(CB * LOCAL * 8, HEAD)
            vf = kin[l, c, 1].astype(F32).reshape(CB * LOCAL * 8, HEAD)
            stage[...] = jnp.concatenate([kf, vf], axis=1)
            for h in range(8):
                rows = stage[pl.ds(h, CB * LOCAL, stride=8), :].astype(BF)
                send[l, h // 2, sl, h % 2] = rows.reshape(CB, LOCAL, 128)
            recv[l, sl, me] = send[l, me, sl]
            if l == 0:
                start_sends(l, c)

    def ars_of(a, n):
        return ars.at[a // 2, n + 1 if a % 2 else 0]

    def ar_start(a, n, width):
        for j in (2, 3, 1):
            sl = pl.ds(n, width)
            pltpu.make_async_remote_copy(
                ar.at[a, me, sl], ar.at[a, me, sl], ass, ars_of(a, n),
                device_id={'tp': peers[j]}, device_id_type=MESH).start()

    def ar_sum(a, h, width):
        parts = []
        for n in range(NCH):
            if n % width == 0:
                all_of(ar.at[a, pl.ds(0, 3), pl.ds(n, width)], ars_of(a, n)).wait()
            tot = ar[a, 0, n].astype(F32)
            for s in range(1, TP):
                tot = tot + ar[a, s, n].astype(F32)
            parts.append(tot)
        return (h.astype(F32) + jnp.concatenate(parts, axis=1)).astype(BF)

    def rms(h, gain):
        hf = h.astype(F32)
        scale = lax.rsqrt(jnp.mean(hf * hf, axis=1, keepdims=True) + EPS)
        return (hf * scale * gain.astype(F32)).astype(BF)

    lane = iota((B, 128), 1)
    low = lane < HEAD

    def rope(x, cosv, sinv):
        rot = jnp.where((lane % HEAD) < HEAD // 2, pltpu.roll(x, 128 - HEAD // 2, 1), pltpu.roll(x, HEAD // 2, 1))
        return (x * cosv + rot * sinv).astype(BF).astype(F32)

    with jax.named_scope('pack0'):
        pack(0)
    for l in range(LAYERS):
        for c in range(WCH):
            for cp in expert_in(l, c):
                cp.start()
        if l == 0:
            for cp in proj_in(1):
                cp.start()
    with jax.named_scope('pack1'):
        pack(1)
    for cp in smalls[:4]:
        cp.wait()
    all_of(g_b, sm.at[4]).wait()
    lenv = jnp.zeros((B, 128), jnp.int32)
    rowi = iota((B, 128), 0)
    for b in range(B):
        lenv = jnp.where(rowi == b, lens_s[b], lenv)
    freq = jnp.exp((lane % (HEAD // 2)).astype(F32) * (-2.0 * math.log(THETA) / HEAD))
    ang = lenv.astype(F32) * freq
    cosv = jnp.cos(ang)
    sinv = jnp.sin(ang)
    sinv = jnp.where((lane % HEAD) < HEAD // 2, -sinv, sinv)

    row64 = iota((64, 128), 0)
    rowb = row64 % B
    col = iota((64, 128), 1)
    pos = (col // 32) * LOCAL + col % LOCAL
    same = ((col // LOCAL) % 2) == (row64 // 32)
    len64 = jnp.concatenate([lenv] * 4, axis=0)
    valid = same & (pos <= len64)
    isnew = same & (pos == len64)
    keep = len64 >= 0
    wide_keep = jnp.concatenate([lenv, lenv], axis=1) >= 0

    def attention(l, h):
        a = rms(h, g_b[0, l:l + 1, :])
        q, kv = jnp.zeros((B, 256), F32), jnp.zeros((B, 256), F32)
        for kk in range(4):
            ks = slice(kk * 256, (kk + 1) * 256)
            kv = kv + dot(a[:, ks], jnp.concatenate([proj_b[l, 2, ks, :], proj_b[l, 3, ks, :]], axis=1))
            q = q + dot(a[:, ks], jnp.concatenate([proj_b[l, 0, ks, :], proj_b[l, 1, ks, :]], axis=1))
        k = rope(kv[:, :128], cosv, sinv)
        v = kv[:, 128:].astype(BF).astype(F32)
        new0 = jnp.where(low, k, pltpu.roll(v, HEAD, 1))
        new1 = jnp.where(low, pltpu.roll(k, HEAD, 1), v)
        kvn[l, 0] = new0
        kvn[l, 1] = new1
        qs = []
        for i in range(2):
            qi = rope(q[:, i * 128:(i + 1) * 128], cosv, sinv)
            qs.append(jnp.where(low, qi, 0.0))
            qs.append(jnp.where(low, pltpu.roll(qi, HEAD, 1), 0.0))
        qf = jnp.concatenate(qs, axis=0)
        newr = jnp.concatenate([new0, new0, new1, new1], axis=0)
        qb = qf.astype(BF)
        snew = jnp.sum(qf * newr, axis=1, keepdims=True)
        s = jnp.zeros((64, 128), F32)
        for c in range(CHUNKS):
            if l == 0:
                kv_wait(l, c, 1)
                if c == 1:
                    start_sends(1, 0)
            for b in range(c * CB, (c + 1) * CB, 2):
                kvb = recv[l, b:b + 2].reshape(256, 128)
                sb = dot_nt(qb, kvb)
                s = jnp.where(rowb == b, sb[:, :128], s)
                s = jnp.where(rowb == b + 1, sb[:, 128:], s)
        s = jnp.where(isnew, snew, s) * (HEAD ** -0.5)
        s = jnp.where(valid, s, -1e30)
        e = jnp.exp(s - jnp.max(s, axis=1, keepdims=True))
        p = (e / jnp.sum(e, axis=1, keepdims=True)).astype(BF).astype(F32)
        pn = jnp.sum(jnp.where(isnew, p, 0.0), axis=1, keepdims=True)
        p = jnp.where(isnew, 0.0, p)
        halves = [pn * newr, jnp.zeros((64, 128), F32)]
        for b in range(0, B, 2):
            pb = jnp.concatenate([jnp.where(rowb == b, p, 0.0), jnp.where(rowb == b + 1, p, 0.0)], axis=1).astype(BF)
            i = b // 2 % 2
            halves[i] = halves[i] + dot(pb, recv[l, b:b + 2].reshape(256, 128))
        o = halves[0] + jnp.where(keep, halves[1], 0.0)
        att = jnp.concatenate(
            [jnp.where(low, pltpu.roll(o[32 * i:32 * i + 16], HEAD, 1), o[32 * i + 16:32 * i + 32]) for i in range(2)],
            axis=1).astype(BF)
        with jax.named_scope('oproj'):
            outs_n = [dot(att, jnp.concatenate([wo_col(l, 2 * n), wo_col(l, 2 * n + 1)], axis=1)) for n in range(NCH)]
            for n in range(NCH):
                ar[2 * l, me, n] = outs_n[n].astype(BF)
            ar_start(2 * l, 0, NCH)

    def write_caches(l, lo, hi):
        row = iota((SEQ, 128), 0)

        def write_row(b, carry):
            kvb = recv[l, b].astype(F32)
            for g in range(2):
                x = kvb[:, g].reshape(SEQ, 128)
                x = jnp.where(row == lens_s[b], kvn[l, g, pl.ds(b, 1), :], x)
                istage[pl.ds(g, SEQ, stride=2), :] = x
            z = istage[...]
            outs[l][0][b] = z[:, :HEAD].astype(BF)
            outs[l][1][b] = z[:, HEAD:].astype(BF)
            return carry

        lax.fori_loop(lo, hi, write_row, 0)

    def chosen(l):
        choice = cho_b[l]
        onehot = jnp.zeros((EXPERTS, B), F32)
        erow = iota((EXPERTS, B), 0)
        for j in range(8):
            onehot = onehot + (erow == choice[j:j + 1, :]).astype(F32)
        eye = (iota((B, B), 0) == iota((B, B), 1)).astype(BF)
        return dot_nt(eye, onehot.astype(BF))

    def gates(l, m, mask):
        mask = mask > 0.5
        logits = jnp.where(mask, dot_nt(m, wr_b[l]), -1e30)
        ex = jnp.where(mask, jnp.exp(logits - jnp.max(logits, axis=1, keepdims=True)), 0.0)
        return ex / jnp.sum(ex, axis=1, keepdims=True)

    def experts(l, h1, mask):
        m = rms(h1, g_b[1, l:l + 1, :])
        gate = gates(l, m, mask)
        for e in range(EXPERTS):
            acc = None
            for kk in range(4):
                ks = slice(kk * 256, (kk + 1) * 256)
                rows = slice(e * D + kk * 256, e * D + (kk + 1) * 256)
                t = dot(m[:, ks], jnp.concatenate([exp_b[l, 0, rows, :], exp_b[l, 1, rows, :]], axis=1))
                acc = t if acc is None else acc + t
            ga_act, up = acc[:, :128], acc[:, 128:]
            act = ga_act * jax.nn.sigmoid(ga_act) * up * gate[:, e:e + 1]
            ub[e] = act.astype(BF)
        with jax.named_scope('down'):
            us = [jnp.concatenate([ub[2 * i], ub[2 * i + 1]], axis=1) for i in range(16)]
            for n in range(NCH):
                halves = [None, None]
                for i in range(16):
                    rows = [slice(c * EXPERTS * 128 + i * 256, c * EXPERTS * 128 + (i + 1) * 256) for c in (2 * n, 2 * n + 1)]
                    t = dot(us[i], jnp.concatenate([exp_b[l, 2, rl, :] for rl in rows], axis=1))
                    halves[i % 2] = t if halves[i % 2] is None else halves[i % 2] + t
                ar[2 * l + 1, me, n] = (jnp.where(wide_keep, halves[0], 0.0) + halves[1]).astype(BF)
                ar_start(2 * l + 1, n, 1)

    h = hid_b[...]
    for l in range(LAYERS):
        proj_wait(l)
        if l == 1:
            kv_wait(l, 0, CHUNKS)
        with jax.named_scope('attention%d' % l):
            attention(l, h)
        mask = chosen(l)
        with jax.named_scope('write_caches'):
            write_caches(l, 0, B // 2)
            if l == 0:
                for c in range(1, CHUNKS):
                    start_sends(1, c)
            write_caches(l, B // 2, B)
        expert_wait(l)
        with jax.named_scope('sum_att'):
            h1 = ar_sum(2 * l, h, NCH)
        with jax.named_scope('experts%d' % l):
            experts(l, h1, mask)
        with jax.named_scope('sum_moe'):
            h = ar_sum(2 * l + 1, h1, 1)
    hst[...] = h
    all_of(send.at[:, pl.ds(0, 3)], ss).wait()
    all_of(ar.at[:, pl.ds(0, 3)], ass).wait()


def write_out(*refs):
    srcs, dsts, sem = refs[:5], refs[5:10], refs[10]
    for s, d, n, i in zip(srcs, dsts, (1, 4, 4, 4, 4), range(5)):
        rows = B // n
        for c in range(n):
            pltpu.make_async_copy(s.at[pl.ds(c * rows, rows)], d.at[pl.ds(c * rows, rows)], sem.at[i]).start()
    for s, d, i in zip(srcs, dsts, range(5)):
        pltpu.make_async_copy(s, d, sem.at[i]).wait()


def solution(mesh):
    seq_spec = P('dp', 'tp', None, None)
    head_spec = P('dp', None, 'tp', None)
    col_spec = P(None, None, 'tp')
    ff_spec = P(None, None, None, 'tp')
    anyspec = pl.BlockSpec(memory_space=pl.ANY)
    dma = pltpu.SemaphoreType.DMA

    def local_step(hidden, lengths, choice, keys_one, vals_one, keys_two, vals_two, g_attn, w_q, w_k, w_v, w_o, g_mlp, w_router, w_gate, w_up, w_down):
        cho = jnp.transpose(choice, (0, 2, 1))
        wr = jnp.transpose(w_router, (0, 2, 1))
        wd = w_down.reshape(LAYERS, EXPERTS * 128, D)
        wg = w_gate.reshape(LAYERS, EXPERTS * D, 128)
        wu = w_up.reshape(LAYERS, EXPERTS * D, 128)
        shapes = ((B, D),) + ((B, SEQ * 2, HEAD),) * 4
        results = pl.pallas_call(
            kernel,
            out_shape=tuple(pltpu.VMEM(s, BF) for s in shapes),
            in_specs=[anyspec] * 17,
            out_specs=(pl.BlockSpec(memory_space=pltpu.VMEM),) * 5,
            scratch_shapes=[
                pltpu.SMEM((B,), jnp.int32),
                pltpu.VMEM((B, D), BF),
                pltpu.VMEM((LAYERS, 8, B), jnp.int32),
                pltpu.VMEM((2, LAYERS, D), BF),
                pltpu.VMEM((LAYERS, 6, D, 128), BF),
                pltpu.VMEM((LAYERS, EXPERTS, D), BF),
                pltpu.VMEM((LAYERS, 3, EXPERTS * D, 128), BF),
                pltpu.VMEM((LAYERS, CHUNKS, 2, CB, LOCAL, 8, HEAD), BF),
                pltpu.VMEM((CB * LOCAL * 8, 128), F32),
                pltpu.VMEM((LAYERS, TP, B, 2, LOCAL, 128), BF),
                pltpu.VMEM((LAYERS, B, TP, 2, LOCAL, 128), BF),
                pltpu.VMEM((2 * SEQ, 128), F32),
                pltpu.VMEM((LAYERS, 2, B, 128), F32),
                pltpu.VMEM((2 * LAYERS, TP, NCH, B, NW), BF),
                pltpu.VMEM((EXPERTS, B, 128), BF),
                dma((5,)),
                dma((CHUNKS + 1,)),
                dma((LAYERS,)),
                dma((LAYERS,)),
                dma,
                dma((CHUNKS + 1,)),
                dma,
                dma((LAYERS, NCH + 1)),
            ],
            compiler_params=pltpu.CompilerParams(collective_id=0, has_side_effects=True, vmem_limit_bytes=63_500_000),
            name='decode_two_layers',
        )(lengths, hidden, cho, keys_one, vals_one, keys_two, vals_two, g_attn, w_q, w_k, w_v, w_o, g_mlp, wr, wg, wu, wd)
        h, k1, v1, k2, v2 = pl.pallas_call(
            write_out,
            out_shape=tuple(jax.ShapeDtypeStruct(s, BF) for s in shapes),
            in_specs=[pl.BlockSpec(memory_space=pltpu.VMEM)] * 5,
            out_specs=(anyspec,) * 5,
            scratch_shapes=[dma((5,))],
            compiler_params=pltpu.CompilerParams(vmem_limit_bytes=1_000_000),
            name='write_out',
        )(*results)
        shape = (B, SEQ, 2, HEAD)
        return (h, k1.reshape(shape), v1.reshape(shape), k2.reshape(shape), v2.reshape(shape))

    return jax.shard_map(local_step, mesh=mesh, in_specs=(P('dp', None), P('dp'), P(None, 'dp', None), seq_spec, seq_spec, seq_spec, seq_spec, P(), col_spec, col_spec, col_spec, P(None, 'tp', None), P(), P(), ff_spec, ff_spec, P(None, None, 'tp', None)), out_specs=(P('dp', None), head_spec, head_spec, head_spec, head_spec), check_vma=False)
```

time: 45.7 us -> 34.6 us (0.76)
  Pallas kernels: 44.9 us -> 33.8 us
    pallas_call x1, Pallas kernels: 43.5 us -> 32.4 us  [local_step(): pl.pallas_call(kernel, out_shape=tuple((pltpu.VMEM(s, BF) for s in shapes...]
where the time goes in v3:
time: 34.6 us; the launch traced here: 34.4 us
  Pallas kernels  33.8 us (98%)
  between operations  0.65 us (2%)
    pallas_call x1, Pallas kernels, local_step(): pl.pallas_call(kernel, out_shape=tuple((pltpu.VMEM(s, BF) for s in shapes...  32.4 us
    pallas_call x1, Pallas kernels, local_step(): pl.pallas_call(write_out, out_shape=tuple((jax.ShapeDtypeStruct(s, BF) fo...  1.35 us

profile of v3, /device:TPU:0, one launch (start us, length us, event | category | flops | bytes accessed | tf_op | source)
XLA Modules:
  0.0 34.4 jit_solution(16413559556669025042)
XLA Ops:
  0.6 32.4 %decode_two_layers.1 = (bf16[16,1024]{1,0:T(8,128)(2,1)S(1)}, bf16[16,128,64]{2,1,0:T(8,128)(2,1)S(1)}, bf16[16,128,64]{2,1,0:T(8,128)(2,1)S(1)}, bf16[16,128,64...) custom-call(s32[16]{0:T(128)} %lens.1, bf16[16,1024]{1,0:T(8,128)(2,1)} %hid.1, s32[2,8,16]{2,1,0:T(8,128)} %bitcast.13, ...), custom_call_target="tpu_custom_call" | custom-call | tf_op jit(solution)/shard_map/decode_two_layers/pallas_call | solution.py:359
  33.1 1.4 %write_out.1 = (bf16[16,1024]{1,0:T(8,128)(2,1)}, bf16[16,128,64]{2,1,0:T(8,128)(2,1)}, bf16[16,128,64]{2,1,0:T(8,128)(2,1)}, bf16[16,128,64]{2,1,0:T(8,128)(2,1)}, bf16[16,128,64]{2,1,0:T(8,128)(2,1)}) custom-call(bf16[16,1024]{1,0:T(8,128)(2,1)S(1)} %get-tuple-element.15.refs_0_, bf16[16,128,64]{2,1,0:T(8,128)(2,1)S(1)} %get-tuple-element.16.refs_1_, ...), custom_call_target="tpu_custom_call" | custom-call | tf_op jit(solution)/shard_map/write_out/pallas_call | solution.py:392
